TPU v7x, 256 devices: a whole 4x4x8 slice. The times are simulated.
256 devices in a mesh: blk: 16 (over x, y_hi, core), grp: 16 (over y_lo, z).
Axes of the slice: x: 4, y: 4 (y_hi: 2, y_lo: 2; y = y_hi * 2 + y_lo), z: 8, core: 2. Of those that a mesh axis runs over, the one named last changes fastest.
Arguments:
- amplitudes: bfloat16 [896, 4, 896], P('blk', None, 'grp'), may hold values from -6 to 6
- grid_factor: bfloat16 [8192, 896], P(('blk', 'grp')), may hold values from -0.1875 to 0.1875
- metric: float32 [8192, 16, 512], P('blk', 'grp'), may hold values from -0.625 to 0.625
- virt_energy: float32 [896], replicated, may hold values from 0.2 to 4
- pair_energy: float32 [4], replicated, may hold values from -2 to -0.5
Outputs:
- residual: float32 [896, 4, 896], P('blk', None, 'grp')
All inputs are finite; a program needn't handle non-finite values.
Results may differ from a plain program's by a relative error of at most 0.005.
Values may be sent and summed in bfloat16 or wider, within the bound.
A program may use at most 64 MiB of HBM per device.

v0:
```python
import jax
import jax.numpy as jnp
from jax import lax
from jax.sharding import Mesh
from jax.sharding import PartitionSpec as P

GRP = ("grp_0", "grp_1")
BLK_GRP = ("blk", "grp_0", "grp_1")


def from_everyone(x, axis):
    count = lax.axis_size(axis)
    return lax.all_to_all(jnp.broadcast_to(x[None], (count, *x.shape)), axis, 0, 0, tiled=True)


def joined_along(pieces, dim):
    shape = list(pieces.shape[1:])
    shape[dim] *= pieces.shape[0]
    return jnp.moveaxis(pieces, 0, dim).reshape(shape)


def gather_directly(x, axis, dim):
    pieces = from_everyone(x, axis)
    return joined_along(pieces, dim)


def stacked_from(x, axes, sequence):
    pieces = x[None]
    for k in sequence:
        pieces = lax.all_gather(pieces, axes[k], axis=0, tiled=True)
    current = [lax.axis_size(axes[k]) for k in reversed(sequence)]
    pieces = pieces.reshape(*current, *x.shape)
    turned = sorted(range(len(sequence)), key=lambda place: sequence[len(sequence) - 1 - place])
    return pieces.transpose(*turned, *range(len(sequence), pieces.ndim)).reshape(-1, *x.shape)


def gather_axes(x, axes, sequence, dim):
    return joined_along(stacked_from(x, axes, sequence), dim)


def own_block(pieces, axes, sequence):
    shape = [lax.axis_size(a) for a in axes]
    pieces = pieces.reshape(*shape, *pieces.shape[1:])
    pieces = pieces.transpose(*sequence, *range(len(axes), pieces.ndim))
    pieces = pieces.reshape(-1, *pieces.shape[len(axes) :])
    for k in sequence:
        pieces = lax.psum_scatter(pieces, axes[k], scatter_dimension=0, tiled=True)
    return pieces[0]


def cut_along(x, dim, count):
    shape = x.shape
    pieces = x.reshape(*shape[:dim], count, shape[dim] // count, *shape[dim + 1 :])
    return jnp.moveaxis(pieces, dim, 0)


def sum_by_axis(x, axes, sequence, dim):
    count = lax.axis_size(axes)
    return own_block(cut_along(x, dim, count), axes, sequence)


def sent_and_summed(x, axis, dim):
    pieces = cut_along(x, dim, lax.axis_size(axis))
    arrived = lax.all_to_all(pieces, axis, split_axis=0, concat_axis=0, tiled=True)
    return arrived.astype(jnp.float32).sum(axis=0)


def local(amplitudes, grid_factor, metric, virt_energy, pair_energy):
    row_factor = gather_directly(grid_factor, GRP, 0)
    column_factor = gather_directly(grid_factor, "blk", 0)
    amplitude_rows = gather_directly(amplitudes, "blk", 0)
    row_count = row_factor.shape[0]
    left_part = jnp.einsum(
        "pc,ckd->kpd", row_factor, amplitude_rows, preferred_element_type=jnp.float32
    ).astype(jnp.bfloat16)
    columns = column_factor
    products = jnp.einsum(
        "kpd,qd->kpq",
        gather_axes(left_part, GRP, (0, 1), 2),
        columns,
        preferred_element_type=jnp.float32,
    )
    weighted = (metric.reshape(row_count, -1)[None] * products).astype(jnp.bfloat16)
    columns = column_factor
    mixed = (
        sum_by_axis(
            jnp.einsum("kpq,qb->bkp", weighted, columns, preferred_element_type=jnp.float32).astype(
                jnp.bfloat16
            ),
            GRP,
            (1, 0),
            0,
        )
        .astype(jnp.float32)
        .astype(jnp.bfloat16)
    )
    columns = row_factor
    ladder = sent_and_summed(
        jnp.einsum("pa,bkp->akb", columns, mixed, preferred_element_type=jnp.float32).astype(
            jnp.bfloat16
        ),
        "blk",
        0,
    )
    first_energy = lax.dynamic_slice_in_dim(
        virt_energy, lax.axis_index("blk") * amplitudes.shape[0], amplitudes.shape[0]
    )
    second_energy = lax.dynamic_slice_in_dim(
        virt_energy, lax.axis_index(GRP) * amplitudes.shape[2], amplitudes.shape[2]
    )
    denominator = (
        first_energy[:, None, None] + second_energy[None, None, :] - pair_energy[None, :, None]
    )
    return denominator * amplitudes.astype(jnp.float32) + ladder


def solution(mesh):
    split = Mesh(mesh.devices.reshape(mesh.shape["blk"], 2, 8), ("blk", "grp_0", "grp_1"))
    in_specs = (P("blk", None, GRP), P(BLK_GRP, None), P("blk", GRP, None), P(), P())
    out_specs = P("blk", None, GRP)
    return jax.shard_map(local, mesh=split, in_specs=in_specs, out_specs=out_specs, check_vma=False)
```

profile of v0, /device:TPU:1, one launch (start us, length us, event | category | flops | bytes accessed | tf_op | source)
XLA Modules:
  0.0 239.4 jit_solution(6617497980471759122)
XLA Ops:
  6.5 0.9 copy.17
  7.5 0.1 broadcast_bitcast_fusion
  7.6 1.5 reshape.67
  9.1 18.4 %all_to_all.20 = bf16[16,2,6272]{2,1,0:T(2,128)(2,1)S(1)} all-to-all(bf16[16,2,6272]{2,1,0:T(2,128)(2,1)S(1)} %reshape.67), channel_id=1, replica_groups=mesh['blk'=16,'grp_0'=2,'grp_1'=8] {'blk'}, dimensions={0} | all-to-all | bytes 802816 | tf_op jit(solution)/shard_map/all_to_all | solution.py:13
  27.5 1.8 broadcast_in_dim.7
  29.3 8.4 %all-to-all-start.1 = ((bf16[16,32,896]{2,1,0:T(8,128)(2,1)}), bf16[16,32,896]{2,1,0:T(8,128)(2,1)S(1)}, u32[]{:S(2)}, u32[]{:S(2)}) async-start(bf16[16,32,896]{2,1,0:T(8,128)(2,1)} %broadcast_in_dim.7), calls=%async_computation.1 | async-start | bytes 1835008 | tf_op jit(solution)/shard_map/all_to_all | solution.py:13
  37.7 0.0 all-gather.3.cloned.1.call-start
  37.8 1.6 reshape.68
  39.4 0.4 copy.19
  39.8 1.1 reshape.56
  40.9 19.1 %all-to-all-done.1 = bf16[16,32,896]{2,1,0:T(8,128)(2,1)S(1)} async-done(((bf16[16,32,896]{2,1,0:T(8,128)(2,1)}), bf16[16,32,896]{2,1,0:T(8,128)(2,1)S(1)}, u32[]{:S(2)}, u32[]{:S(2)}) %all-to-all-start.1) | async-done | bytes 917536 | tf_op jit(solution)/shard_map/all_to_all | solution.py:13
  60.0 0.5 fusion.1
  60.4 5.6 %all-gather = bf16[8,512,56]{1,2,0:T(8,128)(2,1)} all-gather(bf16[4,512,56]{1,2,0:T(8,128)(2,1)S(1)} %fusion.1), channel_id=2, replica_groups=mesh['blk'=16,'grp_0'=2,'grp_1'=8] {'grp_0'}, dimensions={0}, use_global_device_ids=true | all-gather | bytes 688128 | tf_op jit(solution)/shard_map/all_gather | solution.py:30
  66.1 0.0 all-gather.3.cloned.1.call-update
  66.1 7.9 %all-to-all-start.2 = ((bf16[16,32,896]{2,1,0:T(8,128)(2,1)}), bf16[16,32,896]{2,1,0:T(8,128)(2,1)S(1)}, u32[]{:S(2)}, u32[]{:S(2)}) async-start(bf16[16,32,896]{2,1,0:T(8,128)(2,1)} %broadcast_in_dim.7), calls=%async_computation.2 | async-start | bytes 1835008 | tf_op jit(solution)/shard_map/all_to_all | solution.py:13
  74.0 0.0 reduce-scatter.3.cloned.1.call-start
  74.0 1.3 copy.33
  75.3 40.1 %all-gather.3.cloned.1.call-done = bf16[16,4,512,56]{2,3,1,0:T(8,128)(2,1)} async-done(((bf16[2,4,512,56]{2,3,1,0:T(8,128)(2,1)}), bf16[16,4,512,56]{2,3,1,0:T(8,128)(2,1)}) %all-gather.3.cloned.1.call-update) | async-done | bytes 3670032 | tf_op jit(solution)/shard_map/all_gather | solution.py:30
  115.5 2.3 copy.20
  117.8 2.1 copy.21
  119.8 0.0 all-to-all-done.2
  119.8 7.5 %convert_bitcast_fusion = bf16[896,4,512]{0,2,1:T(8,128)(2,1)} fusion(bf16[512,896,1]{1,0,2:T(8,128)(2,1)S(1)} %bitcast.61, bf16[4,512,896]{1,2,0:T(8,128)(2,1)} %bitcast.56, f32[512,512]{1,0:T(8,128)S(1)} %bitcast.60), kind=kOutput, calls=%fused_computation.1 | convolution fusion | flops 3762028544 | bytes 9306112 | tf_op jit(solution)/shard_map/kpq,qb->bkp/dot_general | solution.py:87
  127.4 5.9 %copy.23 = bf16[896,4,512]{2,0,1:T(8,128)(2,1)} copy(bf16[896,4,512]{0,2,1:T(8,128)(2,1)} %convert_bitcast_fusion) | data formatting | bytes 7340032 | tf_op jit(solution)/shard_map/convert_element_type | solution.py:87
  133.3 4.3 %copy.24 = bf16[8,2,56,4,512]{4,2,3,1,0:T(8,128)(2,1)} copy(bf16[8,2,56,4,512]{4,2,0,1,3:T(8,128)(2,1)} %bitcast.52) | data formatting | bytes 7340032 | tf_op jit(solution)/shard_map/transpose | solution.py:44
  137.6 0.0 reduce-scatter.3.cloned.1.call-update
  137.7 0.0 reduce-scatter.5.cloned.1.call-start
  137.7 49.2 %reduce-scatter.3.cloned.1.call-done = bf16[2,56,4,512]{3,1,2,0:T(8,128)(2,1)} async-done(((bf16[16,56,4,512]{3,1,2,0:T(8,128)(2,1)}), bf16[2,56,4,512]{3,1,2,0:T(8,128)(2,1)}) %reduce-scatter.3.cloned.1.call-update) | async-done | bytes 458768 | tf_op jit(solution)/shard_map/reduce_scatter | solution.py:47
  186.9 0.0 reduce-scatter.5.cloned.1.call-update
  186.9 20.5 %reduce-scatter.5.cloned.1.call-done = bf16[1,56,4,512]{3,1,2,0:T(8,128)(2,1)} async-done(((bf16[2,56,4,512]{3,1,2,0:T(8,128)(2,1)}), bf16[1,56,4,512]{3,1,2,0:T(8,128)(2,1)}) %reduce-scatter.5.cloned.1.call-update) | async-done | bytes 229392 | tf_op jit(solution)/shard_map/reduce_scatter | solution.py:47
  207.4 1.4 fusion
  208.8 0.0 copy-start
  208.8 1.5 reshape.63
  210.3 0.2 copy.34
  210.5 2.2 reshape.69
  212.7 7.2 %all-to-all-start.3 = ((bf16[16,2,6272]{2,1,0:T(2,128)(2,1)}), bf16[16,2,6272]{2,1,0:T(2,128)(2,1)S(1)}, u32[]{:S(2)}, u32[]{:S(2)}) async-start(bf16[16,2,6272]{2,1,0:T(2,128)(2,1)} %reshape.69), calls=%async_computation.5 | async-start | bytes 802816 | tf_op jit(solution)/shard_map/all_to_all | solution.py:64
  220.0 0.8 fusion.3
  220.8 0.1 broadcast_add_fusion
  220.9 9.3 %all-to-all-done.3 = bf16[16,2,6272]{2,1,0:T(2,128)(2,1)S(1)} async-done(((bf16[16,2,6272]{2,1,0:T(2,128)(2,1)}), bf16[16,2,6272]{2,1,0:T(2,128)(2,1)S(1)}, u32[]{:S(2)}, u32[]{:S(2)}) %all-to-all-start.3) | async-done | bytes 401440 | tf_op jit(solution)/shard_map/all_to_all | solution.py:64
  230.2 1.6 reshape.70
  231.8 0.2 convert_reduce_fusion
  232.0 0.0 copy-done
  232.0 0.1 multiply_add_fusion
  232.1 0.7 copy.27
Async XLA Ops:
  29.3 30.7 %all-to-all-start.1 = ((bf16[16,32,896]{2,1,0:T(8,128)(2,1)}), bf16[16,32,896]{2,1,0:T(8,128)(2,1)S(1)}, u32[]{:S(2)}, u32[]{:S(2)}) async-start(bf16[16,32,896]{2,1,0:T(8,128)(2,1)} %broadcast_in_dim.7), calls=%async_computation.1 | async-start | bytes 1835008 | tf_op jit(solution)/shard_map/all_to_all | solution.py:13
  37.7 77.8 %all-gather.3.cloned.1.call-start = ((), (), s32[]{:S(2)}) async-start(), calls=%async_computation.6 | async-start | bytes 4128768 | tf_op jit(solution)/shard_map/all_gather | solution.py:30
  66.1 53.7 %all-to-all-start.2 = ((bf16[16,32,896]{2,1,0:T(8,128)(2,1)}), bf16[16,32,896]{2,1,0:T(8,128)(2,1)S(1)}, u32[]{:S(2)}, u32[]{:S(2)}) async-start(bf16[16,32,896]{2,1,0:T(8,128)(2,1)} %broadcast_in_dim.7), calls=%async_computation.2 | async-start | bytes 1835008 | tf_op jit(solution)/shard_map/all_to_all | solution.py:13
  74.0 112.9 %reduce-scatter.3.cloned.1.call-start = ((), (), s32[]{:S(2)}) async-start(), calls=%async_computation.7 | async-start | bytes 4128768 | tf_op jit(solution)/shard_map/reduce_scatter | solution.py:47
  137.7 69.8 %reduce-scatter.5.cloned.1.call-start = ((), (), s32[]{:S(2)}) async-start(), calls=%async_computation.8 | async-start | bytes 688128 | tf_op jit(solution)/shard_map/reduce_scatter | solution.py:47
  208.8 23.2 %copy-start = (f32[4]{0:T(128)S(1)}, f32[4]{0:T(128)}, u32[]{:S(2)}) copy-start(f32[4]{0:T(128)} %param.9) | copy-start | bytes 52
  212.7 17.4 %all-to-all-start.3 = ((bf16[16,2,6272]{2,1,0:T(2,128)(2,1)}), bf16[16,2,6272]{2,1,0:T(2,128)(2,1)S(1)}, u32[]{:S(2)}, u32[]{:S(2)}) async-start(bf16[16,2,6272]{2,1,0:T(2,128)(2,1)} %reshape.69), calls=%async_computation.5 | async-start | bytes 802816 | tf_op jit(solution)/shard_map/all_to_all | solution.py:64
Sparse Core Ops, SparseCore 0:
  66.2 49.2 all-gather.2
  137.8 49.0 reduce-scatter.2
  189.4 17.9 reduce-scatter.4
where the time goes:
time: 240 us; the launch traced here: 239 us
  waiting for transfers between devices  138 us (58%)
  local copies, waits for them, and re-layouts  30.5 us (13%)
  blocking collectives  24 us (10%)
  starting transfers between devices  23.7 us (10%)
  between operations  13.2 us (6%)
  matrix products  9.37 us (4%)
    reduce_scatter x2, waiting for transfers between devices, own_block(): pieces = lax.psum_scatter(pieces, axes[k], scatter_dimension=0, tiled=True)  69.7 us
    all_gather x1, waiting for transfers between devices, stacked_from(): pieces = lax.all_gather(pieces, axes[k], axis=0, tiled=True)  40.1 us
    all_to_all x2, waiting for transfers between devices, from_everyone(): lax.all_to_all(jnp.broadcast_to(x[None], (count, *x.shape)), axis, 0, 0,...  19.1 us
    all_to_all x1, blocking collectives, from_everyone(): lax.all_to_all(jnp.broadcast_to(x[None], (count, *x.shape)), axis, 0, 0,...  18.4 us
    all_to_all x2, starting transfers between devices, from_everyone(): lax.all_to_all(jnp.broadcast_to(x[None], (count, *x.shape)), axis, 0, 0,...  16.3 us
    unnamed x9, local copies, waits for them, and re-layouts  9.32 us
    all_to_all x1, waiting for transfers between devices, sent_and_summed(): lax.all_to_all(pieces, axis, split_axis=0, concat_axis=0, tiled=True)  9.27 us
    dot_general x1, matrix products, local(): jnp.einsum('kpq,qb->bkp', weighted, columns, preferred_element_type=jnp.f...  7.54 us
  transfers between devices with their start and end apart: 6, of which 5 were waited for; matrix products, arithmetic and copies ran while one was open for 4% of the time, Pallas kernels for 0%

commit v1 on v0

--- a/solution.py
+++ b/solution.py
@@ -27,7 +27,8 @@
 def stacked_from(x, axes, sequence):
     pieces = x[None]
     for k in sequence:
-        pieces = lax.all_gather(pieces, axes[k], axis=0, tiled=True)
+        stack = jnp.stack([pieces] * lax.axis_size(axes[k]))
+        pieces = jnp.concatenate(lax.all_to_all(stack, axes[k], 0, 0), axis=0)
     current = [lax.axis_size(axes[k]) for k in reversed(sequence)]
     pieces = pieces.reshape(*current, *x.shape)
     turned = sorted(range(len(sequence)), key=lambda place: sequence[len(sequence) - 1 - place])

time: 240 us -> 297 us (1.24)
  blocking collectives: 24 us -> 115 us
  waiting for transfers between devices: 138 us -> 103 us
    all_to_all x0 -> x2, blocking collectives: none -> 96.5 us  [stacked_from(): pieces = jnp.concatenate(lax.all_to_all(stack, axes[k], 0, 0), axis=0)]
    all_gather x1 -> x0, waiting for transfers between devices: 40.1 us -> none  [stacked_from(): pieces = lax.all_gather(pieces, axes[k], axis=0, tiled=True)]
    all_to_all x2, waiting for transfers between devices: 19.1 us -> 30.2 us  [from_everyone(): lax.all_to_all(jnp.broadcast_to(x[None], (count, *x.shape)), axis, 0, 0,...]
    reduce_scatter x2, waiting for transfers between devices: 69.7 us -> 63.4 us  [own_block(): pieces = lax.psum_scatter(pieces, axes[k], scatter_dimension=0, tiled=True)]
    all_gather x1 -> x0, blocking collectives: 5.64 us -> none  [stacked_from(): pieces = lax.all_gather(pieces, axes[k], axis=0, tiled=True)]
    unnamed x9 -> x11, local copies, waits for them, and re-layouts: 9.32 us -> 8.12 us
  transfers between devices with their start and end apart: 6 -> 5, of which waited for: 5 -> 5; matrix products, arithmetic and copies ran while one was open for 4% -> 3% of each run, Pallas kernels for 0% -> 0%
where the time goes in v1:
time: 297 us; the launch traced here: 296 us
  blocking collectives  115 us (39%)
  waiting for transfers between devices  103 us (35%)
  local copies, waits for them, and re-layouts  29.6 us (10%)
  starting transfers between devices  23.7 us (8%)
  between operations  13.6 us (5%)
  matrix products  10.8 us (4%)
    all_to_all x2, blocking collectives, stacked_from(): pieces = jnp.concatenate(lax.all_to_all(stack, axes[k], 0, 0), axis=0)  96.5 us
    reduce_scatter x2, waiting for transfers between devices, own_block(): pieces = lax.psum_scatter(pieces, axes[k], scatter_dimension=0, tiled=True)  63.4 us
    all_to_all x2, waiting for transfers between devices, from_everyone(): lax.all_to_all(jnp.broadcast_to(x[None], (count, *x.shape)), axis, 0, 0,...  30.2 us
    all_to_all x1, blocking collectives, from_everyone(): lax.all_to_all(jnp.broadcast_to(x[None], (count, *x.shape)), axis, 0, 0,...  18.4 us
    all_to_all x2, starting transfers between devices, from_everyone(): lax.all_to_all(jnp.broadcast_to(x[None], (count, *x.shape)), axis, 0, 0,...  16.2 us
    all_to_all x1, waiting for transfers between devices, sent_and_summed(): lax.all_to_all(pieces, axis, split_axis=0, concat_axis=0, tiled=True)  9.27 us
    dot_general x1, matrix products, local(): jnp.einsum('kpq,qb->bkp', weighted, columns, preferred_element_type=jnp.f...  8.97 us
    unnamed x11, local copies, waits for them, and re-layouts  8.12 us
  transfers between devices with their start and end apart: 5, of which 5 were waited for; matrix products, arithmetic and copies ran while one was open for 3% of the time, Pallas kernels for 0%

profile of v1, /device:TPU:1, one launch (start us, length us, event | category | flops | bytes accessed | tf_op | source)
XLA Modules:
  0.0 296.0 jit_solution(8276190530892608864)
XLA Ops:
  6.5 0.9 copy.17
  7.5 0.1 broadcast_bitcast_fusion
  7.6 1.5 reshape.64
  9.1 18.4 %all_to_all.30 = bf16[16,2,6272]{2,1,0:T(2,128)(2,1)S(1)} all-to-all(bf16[16,2,6272]{2,1,0:T(2,128)(2,1)S(1)} %reshape.64), channel_id=1, replica_groups=mesh['blk'=16,'grp_0'=2,'grp_1'=8] {'blk'}, dimensions={0} | all-to-all | bytes 802816 | tf_op jit(solution)/shard_map/all_to_all | solution.py:13
  27.5 1.8 broadcast_in_dim.5
  29.3 8.4 %all-to-all-start.1 = ((bf16[16,32,896]{2,1,0:T(8,128)(2,1)}), bf16[16,32,896]{2,1,0:T(8,128)(2,1)S(1)}, u32[]{:S(2)}, u32[]{:S(2)}) async-start(bf16[16,32,896]{2,1,0:T(8,128)(2,1)} %broadcast_in_dim.5), calls=%async_computation.1 | async-start | bytes 1835008 | tf_op jit(solution)/shard_map/all_to_all | solution.py:13
  37.7 1.6 reshape.65
  39.3 0.4 copy.19
  39.7 1.1 reshape.55
  40.8 19.1 %all-to-all-done.1 = bf16[16,32,896]{2,1,0:T(8,128)(2,1)S(1)} async-done(((bf16[16,32,896]{2,1,0:T(8,128)(2,1)}), bf16[16,32,896]{2,1,0:T(8,128)(2,1)S(1)}, u32[]{:S(2)}, u32[]{:S(2)}) %all-to-all-start.1) | async-done | bytes 917536 | tf_op jit(solution)/shard_map/all_to_all | solution.py:13
  59.9 0.5 fusion.1
  60.5 7.5 %all_to_all.31 = bf16[2,1,4,512,56]{3,4,2,1,0:T(8,128)(2,1)S(1)} all-to-all(bf16[2,1,4,512,56]{3,4,2,1,0:T(8,128)(2,1)S(1)} %pad_maximum_fusion), channel_id=1, replica_groups=mesh['blk'=16,'grp_0'=2,'grp_1'=8] {'grp_0'}, dimensions={0} | all-to-all | bytes 917504 | tf_op jit(solution)/shard_map/all_to_all | solution.py:31
  68.0 0.4 stack.7
  68.3 0.0 copy-start
  68.3 89.1 %all_to_all.32 = bf16[8,2,4,512,56]{3,4,2,1,0:T(8,128)(2,1)} all-to-all(bf16[8,2,4,512,56]{3,4,2,1,0:T(8,128)(2,1)S(1)} %stack.7), channel_id=1, replica_groups=mesh['blk'=16,'grp_0'=2,'grp_1'=8] {'grp_1'}, dimensions={0} | all-to-all | bytes 7340032 | tf_op jit(solution)/shard_map/all_to_all | solution.py:31
  157.4 7.8 %all-to-all-start.4 = ((bf16[16,32,896]{2,1,0:T(8,128)(2,1)}), bf16[16,32,896]{2,1,0:T(8,128)(2,1)}, u32[]{:S(2)}, u32[]{:S(2)}) async-start(bf16[16,32,896]{2,1,0:T(8,128)(2,1)} %broadcast_in_dim.5), calls=%async_computation.4 | async-start | bytes 1835008 | tf_op jit(solution)/shard_map/all_to_all | solution.py:13
  165.2 0.0 reduce-scatter.3.cloned.1.call-start
  165.3 0.0 copy-done
  165.3 0.1 copy.33
  165.3 2.3 copy.20
  167.6 2.1 copy.21
  169.7 11.1 %all-to-all-done.4 = bf16[16,32,896]{2,1,0:T(8,128)(2,1)} async-done(((bf16[16,32,896]{2,1,0:T(8,128)(2,1)}), bf16[16,32,896]{2,1,0:T(8,128)(2,1)}, u32[]{:S(2)}, u32[]{:S(2)}) %all-to-all-start.4) | async-done | bytes 917536 | tf_op jit(solution)/shard_map/all_to_all | solution.py:13
  180.8 9.0 %convert_bitcast_fusion = bf16[896,4,512]{0,2,1:T(8,128)(2,1)} fusion(bf16[512,896,1]{1,0,2:T(8,128)(2,1)} %bitcast.10, bf16[4,512,896]{1,2,0:T(8,128)(2,1)} %bitcast.56, f32[512,512]{1,0:T(8,128)S(1)} %bitcast.60), kind=kOutput, calls=%fused_computation.1 | convolution fusion | flops 3762028544 | bytes 9306112 | tf_op jit(solution)/shard_map/kpq,qb->bkp/dot_general | solution.py:88
  189.8 5.9 %copy.23 = bf16[896,4,512]{2,0,1:T(8,128)(2,1)} copy(bf16[896,4,512]{0,2,1:T(8,128)(2,1)} %convert_bitcast_fusion) | data formatting | bytes 7340032 | tf_op jit(solution)/shard_map/convert_element_type | solution.py:88
  195.7 4.3 %copy.24 = bf16[8,2,56,4,512]{4,2,3,1,0:T(8,128)(2,1)} copy(bf16[8,2,56,4,512]{4,2,0,1,3:T(8,128)(2,1)} %bitcast.53) | data formatting | bytes 7340032 | tf_op jit(solution)/shard_map/transpose | solution.py:45
  200.0 0.0 reduce-scatter.3.cloned.1.call-update
  200.1 0.2 reduce-scatter.5.cloned.1.call-start
  200.3 43.0 %reduce-scatter.3.cloned.1.call-done = bf16[2,56,4,512]{3,1,2,0:T(8,128)(2,1)} async-done(((bf16[16,56,4,512]{3,1,2,0:T(8,128)(2,1)}), bf16[2,56,4,512]{3,1,2,0:T(8,128)(2,1)}) %reduce-scatter.3.cloned.1.call-update) | async-done | bytes 458768 | tf_op jit(solution)/shard_map/reduce_scatter | solution.py:48
  243.2 0.0 reduce-scatter.5.cloned.1.call-update
  243.3 20.5 %reduce-scatter.5.cloned.1.call-done = bf16[1,56,4,512]{3,1,2,0:T(8,128)(2,1)} async-done(((bf16[2,56,4,512]{3,1,2,0:T(8,128)(2,1)}), bf16[1,56,4,512]{3,1,2,0:T(8,128)(2,1)}) %reduce-scatter.5.cloned.1.call-update) | async-done | bytes 229392 | tf_op jit(solution)/shard_map/reduce_scatter | solution.py:48
  263.7 1.4 fusion
  265.1 0.0 copy-start.1
  265.1 1.5 reshape.61
  266.6 0.2 copy.34
  266.8 2.2 reshape.66
  269.1 7.2 %all-to-all-start.5 = ((bf16[16,2,6272]{2,1,0:T(2,128)(2,1)}), bf16[16,2,6272]{2,1,0:T(2,128)(2,1)S(1)}, u32[]{:S(2)}, u32[]{:S(2)}) async-start(bf16[16,2,6272]{2,1,0:T(2,128)(2,1)} %reshape.66), calls=%async_computation.7 | async-start | bytes 802816 | tf_op jit(solution)/shard_map/all_to_all | solution.py:65
  276.3 0.8 fusion.3
  277.2 0.1 broadcast_add_fusion
  277.2 9.3 %all-to-all-done.5 = bf16[16,2,6272]{2,1,0:T(2,128)(2,1)S(1)} async-done(((bf16[16,2,6272]{2,1,0:T(2,128)(2,1)}), bf16[16,2,6272]{2,1,0:T(2,128)(2,1)S(1)}, u32[]{:S(2)}, u32[]{:S(2)}) %all-to-all-start.5) | async-done | bytes 401440 | tf_op jit(solution)/shard_map/all_to_all | solution.py:65
  286.5 1.6 reshape.67
  288.1 0.2 convert_reduce_fusion
  288.3 0.0 copy-done.1
  288.3 0.1 multiply_add_fusion
  288.4 0.7 copy.27
  (1 shorter events, 0.0 us)
Async XLA Ops:
  29.3 30.7 %all-to-all-start.1 = ((bf16[16,32,896]{2,1,0:T(8,128)(2,1)}), bf16[16,32,896]{2,1,0:T(8,128)(2,1)S(1)}, u32[]{:S(2)}, u32[]{:S(2)}) async-start(bf16[16,32,896]{2,1,0:T(8,128)(2,1)} %broadcast_in_dim.5), calls=%async_computation.1 | async-start | bytes 1835008 | tf_op jit(solution)/shard_map/all_to_all | solution.py:13
  68.3 96.9 %copy-start = (f32[512,1,512]{2,1,0:T(1,128)S(1)}, f32[512,1,512]{2,1,0:T(1,128)}, u32[]{:S(2)}) copy-start(f32[512,1,512]{2,1,0:T(1,128)} %param.7) | copy-start | bytes 3145732
  157.4 23.4 %all-to-all-start.4 = ((bf16[16,32,896]{2,1,0:T(8,128)(2,1)}), bf16[16,32,896]{2,1,0:T(8,128)(2,1)}, u32[]{:S(2)}, u32[]{:S(2)}) async-start(bf16[16,32,896]{2,1,0:T(8,128)(2,1)} %broadcast_in_dim.5), calls=%async_computation.4 | async-start | bytes 1835008 | tf_op jit(solution)/shard_map/all_to_all | solution.py:13
  165.2 78.0 %reduce-scatter.3.cloned.1.call-start = ((), (), s32[]{:S(2)}) async-start(), calls=%async_computation.8 | async-start | bytes 4128768 | tf_op jit(solution)/shard_map/reduce_scatter | solution.py:48
  200.1 63.7 %reduce-scatter.5.cloned.1.call-start = ((), (), s32[]{:S(2)}) async-start(), calls=%async_computation.9 | async-start | bytes 688128 | tf_op jit(solution)/shard_map/reduce_scatter | solution.py:48
  265.1 23.2 %copy-start.1 = (f32[4]{0:T(128)S(1)}, f32[4]{0:T(128)}, u32[]{:S(2)}) copy-start(f32[4]{0:T(128)} %param.9) | copy-start | bytes 52
  269.1 17.4 %all-to-all-start.5 = ((bf16[16,2,6272]{2,1,0:T(2,128)(2,1)}), bf16[16,2,6272]{2,1,0:T(2,128)(2,1)S(1)}, u32[]{:S(2)}, u32[]{:S(2)}) async-start(bf16[16,2,6272]{2,1,0:T(2,128)(2,1)} %reshape.66), calls=%async_computation.7 | async-start | bytes 802816 | tf_op jit(solution)/shard_map/all_to_all | solution.py:65
Sparse Core Ops, SparseCore 0:
  200.2 43.0 reduce-scatter.2
  245.8 17.9 reduce-scatter.4
